TPU v7x, 256 devices: a whole 4x4x8 slice. The times are simulated.
256 devices in a mesh: dp: 32 (over x, z_lo, core), sub: 8 (over z_hi, y).
Axes of the slice: x: 4, y: 4, z: 8 (z_hi: 2, z_lo: 4; z = z_hi * 4 + z_lo), core: 2. Of those that a mesh axis runs over, the one named last changes fastest.
Arguments:
- context: bfloat16 [403456, 1024], P(('dp', 'sub')), may hold values from -6 to 6
- target: bfloat16 [403456, 1024], P(('dp', 'sub')), may hold values from -16 to 16
- weight: float32 [1024, 1024], P(('dp', 'sub')), may hold values from -0.1875 to 0.1875
- stale: bfloat16 [256, 1024, 1024], P(('dp', 'sub')), may hold values from -1.25 to 1.25
- trigger: int32 [256, 16], P(('dp', 'sub')), may hold values 0 or 1
- aggregate: float32 [1024, 1024], P(('dp', 'sub')), may hold values from -3 to 3
- moment: float32 [1024, 1024], P(('dp', 'sub')), may hold values from -0.6 to 0.6
- second: float32 [1024, 1024], P(('dp', 'sub')), may hold values from 0.0001 to 0.01
Outputs:
- aggregate_new: float32 [1024, 1024], P(('dp', 'sub'))
- weight_new: float32 [1024, 1024], P(('dp', 'sub'))
- moment_new: float32 [1024, 1024], P(('dp', 'sub'))
- second_new: float32 [1024, 1024], P(('dp', 'sub'))
- stale_new: bfloat16 [256, 1024, 1024], P(('dp', 'sub'))
- norms: float32 [16], replicated
All inputs are finite; a program needn't handle non-finite values. No bound on the sum of `trigger` on one device may be relied on, other than what follows from the above.
Results may differ from a plain program's by a relative error of at most 0.006.
Values may be sent and summed in bfloat16 or wider, within the bound.
A program may use at most 64 MiB of HBM per device.

v0:
```python
import functools

import jax
import jax.numpy as jnp
from jax import lax
from jax.sharding import Mesh
from jax.sharding import PartitionSpec as P

SUB = ("sub_0", "sub_1")
DP = ("dp_0", "dp_1", "dp_2")
DP_SUB = ("dp_0", "dp_1", "dp_2", "sub_0", "sub_1")


def laid_out(pieces, dim):
    lengths = list(pieces.shape[1:])
    lengths[dim] *= pieces.shape[0]
    return jnp.moveaxis(pieces, 0, dim).reshape(lengths)


def sent_to_all(value, axis):
    copies = jnp.broadcast_to(value, (lax.axis_size(axis), *value.shape))
    return lax.all_to_all(copies, axis, split_axis=0, concat_axis=0, tiled=True)


def gathered_copies(value, axis, dim):
    return laid_out(sent_to_all(value, axis), dim)


def one_axis_at_a_time(value, axes):
    return functools.reduce(lax.psum, axes, value)


def in_blocks(value, dim, devices):
    lengths = value.shape
    pieces = value.reshape(*lengths[:dim], devices, lengths[dim] // devices, *lengths[dim + 1 :])
    return jnp.moveaxis(pieces, dim, 0)


def sent_and_summed(value, axis, dim):
    pieces = in_blocks(value, dim, lax.axis_size(axis))
    arrived = lax.all_to_all(pieces, axis, split_axis=0, concat_axis=0, tiled=True)
    return arrived.astype(jnp.float32).sum(axis=0)


def body(context, target, weight, stale, trigger, aggregate, moment, second):
    rows = context.shape[0]
    width = context.shape[1]
    owned = weight.shape[0]
    blocks = trigger.shape[1]
    span = width // blocks
    low_rows = weight.astype(jnp.bfloat16)
    low_group = gathered_copies(low_rows, SUB, 0)
    low_whole = lax.all_gather(low_group, DP, axis=0, tiled=True)
    output = jnp.dot(context, low_whole, preferred_element_type=jnp.float32)
    error = (output - target.astype(jnp.float32)).astype(jnp.bfloat16)
    grad = (
        lax.dot_general(
            context, error, (((0,), (0,)), ((), ())), preferred_element_type=jnp.float32
        )
        / rows
    )
    old = stale[0].astype(jnp.float32)
    flags = trigger[0].astype(jnp.float32)[:, None, None]
    blocked = (grad - old).reshape(blocks, span, width)
    squares = jnp.sum(blocked * blocked, axis=(1, 2))
    chosen = (blocked * flags).reshape(width, width)
    fresh = flags * grad.reshape(blocks, span, width) + (1.0 - flags) * old.reshape(
        blocks, span, width
    )
    stale_new = fresh.reshape(1, width, width).astype(jnp.bfloat16)
    norms = one_axis_at_a_time(squares, DP_SUB)
    count_dp = lax.axis_size(DP)
    count_sub = lax.axis_size(SUB)
    layered = chosen.reshape(count_dp, count_sub, owned, width)
    partial_sum = sent_and_summed(layered.astype(jnp.bfloat16), SUB, 1)
    summed = sent_and_summed(partial_sum.astype(jnp.bfloat16), DP, 0).reshape(owned, width)
    aggregate_new = aggregate + summed
    moment_new = 0.9 * moment + 0.1 * aggregate_new
    second_new = 0.999 * second + 0.001 * aggregate_new * aggregate_new
    weight_new = weight - 0.001 * (moment_new / (jnp.sqrt(second_new) + 1e-08) + 0.05 * weight)
    return (aggregate_new, weight_new, moment_new, second_new, stale_new, norms)


def solution(mesh):
    torus = Mesh(mesh.devices.reshape(4, 4, 2, 2, 4), ("dp_0", "dp_1", "dp_2", "sub_0", "sub_1"))
    placed = (
        P(DP_SUB, None),
        P(DP_SUB, None),
        P(DP_SUB, None),
        P(DP_SUB, None, None),
        P(DP_SUB, None),
        P(DP_SUB, None),
        P(DP_SUB, None),
        P(DP_SUB, None),
    )
    return jax.shard_map(
        body,
        mesh=torus,
        in_specs=placed,
        out_specs=(
            P(DP_SUB, None),
            P(DP_SUB, None),
            P(DP_SUB, None),
            P(DP_SUB, None),
            P(DP_SUB, None, None),
            P(),
        ),
        check_vma=False,
    )
```

profile of v0, /device:TPU:8, one launch (start us, length us, event | category | flops | bytes accessed | tf_op | source)
XLA Modules:
  0.0 231.7 jit_solution(8657969876965599879)
XLA Ops:
  7.2 0.0 copy-start
  7.2 0.0 all-gather.2.cloned.1.call-start
  7.2 0.9 convert_element_type.51
  8.1 20.3 %all_to_all.15 = bf16[8,4,1024]{2,1,0:T(4,128)(2,1)S(1)} all-to-all(bf16[8,4,1024]{2,1,0:T(4,128)(2,1)S(1)} %broadcast_in_dim.4), channel_id=1, replica_groups=mesh['dp_0'=4,'dp_1'=4,'dp_2'=2,'sub_0'=2,'sub_1'=4] {'sub_0','sub_1'}, dimensions={0} | all-to-all | bytes 131072 | tf_op jit(solution)/shard_map/all_to_all | solution.py:22
  28.4 0.6 reshape.67
  29.0 0.0 all-gather.2.cloned.1.call-update
  29.1 0.7 broadcast_multiply_fusion
  29.7 0.1 mul.107
  29.8 0.1 mul.108
  29.9 0.7 convert_bitcast_fusion
  30.5 0.1 mul.90
  30.6 0.1 mul.91
  30.7 0.1 mul.112
  30.8 0.1 mul.113
  30.8 54.6 %all-gather.2.cloned.1.call-done = bf16[1024,1024]{1,0:T(8,128)(2,1)} async-done(((bf16[32,1024]{1,0:T(8,128)(2,1)}), bf16[1024,1024]{1,0:T(8,128)(2,1)}) %all-gather.2.cloned.1.call-update) | async-done | bytes 2097168 | tf_op jit(solution)/shard_map/all_gather | solution.py:53
  85.5 14.1 %multiply_reduce_fusion = (f32[1024]{0:T(1024)S(1)}, f32[1024,1024]{1,0:T(8,128)}, bf16[1,1024,1024]{2,1,0:T(8,128)(2,1)}) fusion(bf16[1,1024,1024]{2,1,0:T(8,128)(2,1)} %param.11, f32[1024]{0:T(1024)S(1)} %mul.113, f32[1024]{0:T(1024)S(1)} %mul.108, bf16[1576,1024]{1,0:T(8,128)(2,1)S(1)} %copy-done, bf16[1576,1024]{1,0:T(8,128)(2,1)} %param.9, ...), kind=kOutput, calls=%fused_computation.7 | convolution fusion | flops 6624500736 | bytes 16953344 | tf_op jit(solution)/shard_map/dot_general | solution.py:57
  99.6 5.2 %reshape.68 = f32[32,8,1,4,1024]{4,3,1,0,2:T(4,128)} reshape(f32[1024,1024]{1,0:T(8,128)} %get-tuple-element.7) | data formatting | bytes 8388608 | tf_op jit(solution)/shard_map/reshape | solution.py:64
  104.7 4.7 %fusion.3 = bf16[8,32,1,4,1024]{4,0,3,2,1:T(8,128)(2,1)S(1)} fusion(f32[32,8,1,4,1024]{4,3,1,0,2:T(4,128)} %reshape.68, f32[32]{0:T(128)S(1)} %mul.91), kind=kLoop, calls=%fused_computation.8 | loop fusion | flops 2097152 | bytes 6291584 | tf_op jit(solution)/shard_map/transpose | solution.py:36
  109.4 1.6 copy.18
  111.1 0.0 copy-start.3
  111.1 58.8 %all_to_all.16 = bf16[8,32,1,4,1024]{4,3,1,2,0:T(4,128)(2,1)} all-to-all(bf16[8,32,1,4,1024]{4,3,1,2,0:T(4,128)(2,1)S(1)} %copy.18), channel_id=1, replica_groups=mesh['dp_0'=4,'dp_1'=4,'dp_2'=2,'sub_0'=2,'sub_1'=4] {'sub_0','sub_1'}, dimensions={0} | all-to-all | bytes 4194304 | tf_op jit(solution)/shard_map/all_to_all | solution.py:41
  169.9 3.3 %reduce_sum.37 = bf16[32,4,1024]{2,1,0:T(4,128)(2,1)} reduce(bf16[8,32,1,4,1024]{4,3,1,2,0:T(4,128)(2,1)} %all_to_all.16, bf16[]{:T(256)} %constant.3.clone.1), dimensions={0,2}, to_apply=%region_0.0 | reduce | flops 917504 | bytes 2359298 | tf_op jit(solution)/shard_map/reduce_sum | solution.py:42
  173.3 6.1 %all-to-all-start.2 = ((bf16[32,1,1,4,1024]{4,3,2,1,0:T(4,128)(2,1)}), bf16[32,1,1,4,1024]{4,3,2,1,0:T(4,128)(2,1)S(1)}, u32[]{:S(2)}, u32[]{:S(2)}) async-start(bf16[32,1,1,4,1024]{4,3,2,1,0:T(4,128)(2,1)} %bitcast.4), calls=%async_computation.2 | async-start | bytes 524288 | tf_op jit(solution)/shard_map/all_to_all | solution.py:41
  179.4 0.1 reduce_sum.40
  179.5 0.1 reduce_sum.41
  179.6 10.8 %psum.35 = f32[16]{0:T(128)S(1)} all-reduce(f32[16]{0:T(128)S(1)} %reduce_sum.41), channel_id=1, replica_groups=mesh['dp_0'=4,'dp_1'=4,'dp_2'=2,'sub_0'=2,'sub_1'=4] {'dp_0'}, use_global_device_ids=true, to_apply=%region_4.0 | all-reduce | flops 16 | bytes 128 | tf_op jit(solution)/shard_map/psum | solution.py:30
  190.4 11.6 %psum.36 = f32[16]{0:T(128)S(1)} all-reduce(f32[16]{0:T(128)S(1)} %psum.35), channel_id=1, replica_groups=mesh['dp_0'=4,'dp_1'=4,'dp_2'=2,'sub_0'=2,'sub_1'=4] {'dp_1'}, use_global_device_ids=true, to_apply=%region_5.0 | all-reduce | flops 16 | bytes 128 | tf_op jit(solution)/shard_map/psum | solution.py:30
  202.0 2.5 %psum.37 = f32[16]{0:T(128)S(1)} all-reduce(f32[16]{0:T(128)S(1)} %psum.36), channel_id=1, replica_groups=mesh['dp_0'=4,'dp_1'=4,'dp_2'=2,'sub_0'=2,'sub_1'=4] {'dp_2'}, use_global_device_ids=true, to_apply=%region_6.0 | all-reduce | flops 16 | bytes 128 | tf_op jit(solution)/shard_map/psum | solution.py:30
  204.5 8.8 %psum.38 = f32[16]{0:T(128)S(1)} all-reduce(f32[16]{0:T(128)S(1)} %psum.37), channel_id=1, replica_groups=mesh['dp_0'=4,'dp_1'=4,'dp_2'=2,'sub_0'=2,'sub_1'=4] {'sub_0'}, use_global_device_ids=true, to_apply=%region_7.0 | all-reduce | flops 16 | bytes 128 | tf_op jit(solution)/shard_map/psum | solution.py:30
  213.3 10.0 %psum.39 = f32[16]{0:T(128)} all-reduce(f32[16]{0:T(128)S(1)} %psum.38), channel_id=1, replica_groups=mesh['dp_0'=4,'dp_1'=4,'dp_2'=2,'sub_0'=2,'sub_1'=4] {'sub_1'}, use_global_device_ids=true, to_apply=%region_8.9 | all-reduce | flops 16 | bytes 128 | tf_op jit(solution)/shard_map/psum | solution.py:30
  223.3 0.1 convert_reduce_fusion
  223.4 1.4 multiply_subtract_fusion
  (8 shorter events, 0.0 us)
Async XLA Ops:
  7.2 78.3 %copy-start = (bf16[1576,1024]{1,0:T(8,128)(2,1)S(1)}, bf16[1576,1024]{1,0:T(8,128)(2,1)}, u32[]{:S(2)}) copy-start(bf16[1576,1024]{1,0:T(8,128)(2,1)} %param.8) | copy-start | bytes 9682948
  7.2 78.3 %all-gather.2.cloned.1.call-start = ((), (), s32[]{:S(2)}) async-start(), calls=%async_computation.3 | async-start | bytes 2162688 | tf_op jit(solution)/shard_map/all_gather | solution.py:53
  111.1 112.4 %copy-start.1 = (f32[4,1024]{1,0:T(4,128)S(1)}, f32[4,1024]{1,0:T(4,128)}, u32[]{:S(2)}) copy-start(f32[4,1024]{1,0:T(4,128)} %param.10) | copy-start | bytes 49156
  111.1 112.4 %copy-start.2 = (f32[4,1024]{1,0:T(4,128)S(1)}, f32[4,1024]{1,0:T(4,128)}, u32[]{:S(2)}) copy-start(f32[4,1024]{1,0:T(4,128)} %param.15) | copy-start | bytes 49156
  111.1 112.4 %copy-start.3 = (f32[4,1024]{1,0:T(4,128)S(1)}, f32[4,1024]{1,0:T(4,128)}, u32[]{:S(2)}) copy-start(f32[4,1024]{1,0:T(4,128)} %param.14) | copy-start | bytes 49156
  173.3 50.0 %all-to-all-start.2 = ((bf16[32,1,1,4,1024]{4,3,2,1,0:T(4,128)(2,1)}), bf16[32,1,1,4,1024]{4,3,2,1,0:T(4,128)(2,1)S(1)}, u32[]{:S(2)}, u32[]{:S(2)}) async-start(bf16[32,1,1,4,1024]{4,3,2,1,0:T(4,128)(2,1)} %bitcast.4), calls=%async_computation.2 | async-start | bytes 524288 | tf_op jit(solution)/shard_map/all_to_all | solution.py:41
Sparse Core Ops, SparseCore 0:
  29.2 56.2 all-gather.1
where the time goes:
time: 232 us
  blocking collectives  123 us (53%)
  waiting for transfers between devices  54.6 us (24%)
  matrix products  14.1 us (6%)
  between operations  14.1 us (6%)
  other arithmetic  11.8 us (5%)
  local copies, waits for them, and re-layouts  8 us (3%)
  starting transfers between devices  6.18 us (3%)
    all_to_all x1, blocking collectives, sent_and_summed(): lax.all_to_all(pieces, axis, split_axis=0, concat_axis=0, tiled=True)  58.8 us
    all_gather x1, waiting for transfers between devices, body(): low_whole = lax.all_gather(low_group, DP, axis=0, tiled=True)  54.6 us
    psum x5, blocking collectives, one_axis_at_a_time(): return functools.reduce(lax.psum, axes, value)  43.7 us
    all_to_all x1, blocking collectives, sent_to_all(): return lax.all_to_all(copies, axis, split_axis=0, concat_axis=0, tiled=True)  20.3 us
    dot_general x1, matrix products, body(): lax.dot_general(context, error, (((0,), (0,)), ((), ())), preferred_eleme...  14.1 us
    all_to_all x1, starting transfers between devices, sent_and_summed(): lax.all_to_all(pieces, axis, split_axis=0, concat_axis=0, tiled=True)  6.14 us
    reshape x1, local copies, waits for them, and re-layouts, body(): blocked = (grad - old).reshape(blocks, span, width)  5.17 us
    transpose x1, other arithmetic, in_blocks(): return jnp.moveaxis(pieces, dim, 0)  4.68 us
  transfers between devices with their start and end apart: 2, of which 1 were waited for; matrix products, arithmetic and copies ran while one was open for 1% of the time, Pallas kernels for 0%

commit v1 on v0

v1 whole, which is shorter than its diff:
```python
import functools

import jax
import jax.numpy as jnp
from jax import lax
from jax.experimental import pallas as pl
from jax.experimental.pallas import tpu as pltpu
from jax.sharding import PartitionSpec as P

MESH = pl.DeviceIdType.MESH
F32 = jnp.float32
BF16 = jnp.bfloat16
CHUNKS = 4
NX = 4
NY = 4
NZ = 8
PIECE = 4


def step_kernel(
    rows,
    padded,
    context,
    target,
    weight,
    stale,
    trigger,
    summed_out,
    stale_out,
    norms_out,
    cbuf,
    ct,
    tbuf,
    sbuf,
    fbuf,
    perm,
    perm_t,
    wz,
    wz32,
    wbuf,
    wn,
    ebuf,
    half,
    drecv,
    asend,
    arecv,
    bsend,
    brecv,
    zsend,
    zrecv,
    sqacc,
    nrm,
    nx_buf,
    ny_buf,
    nz_buf,
    cin_sem,
    tin_sem,
    sin_sem,
    fout_sem,
    gz_s,
    gz_r,
    gb_s,
    gb_r,
    ga_s,
    ga_r,
    gd_s,
    gd_r,
    rd_s,
    rd_r,
    ra_s,
    ra_r,
    rb_s,
    rb_r,
    rz_s,
    rz_r,
    n_s,
    n_r,
):
    width = context.shape[1]
    cols = width // CHUNKS
    dp = lax.axis_index("dp")
    sub = lax.axis_index("sub")
    c = lax.rem(dp, 2)
    x = lax.div(dp, 8)
    zlo = lax.rem(lax.div(dp, 2), 4)
    zhi = lax.div(sub, NY)
    y = lax.rem(sub, NY)
    z = zhi * 4 + zlo
    am = x * (1 - c) + y * c
    bm = y * (1 - c) + x * c

    def device(px, py, pz, pc):
        return ((px * 4 + lax.rem(pz, 4)) * 2 + pc, lax.div(pz, 4) * NY + py)

    def a_peer(a):
        return device(a * (1 - c) + x * c, y * (1 - c) + a * c, z, c)

    def b_peer(b):
        return device(x * (1 - c) + b * c, b * (1 - c) + y * c, z, c)

    def x_peer(k):
        return device(lax.rem(x + k, NX), y, z, c)

    def y_peer(k):
        return device(x, lax.rem(y + k, NY), z, c)

    def z_peer(k):
        return device(x, y, lax.rem(z + k, NZ), c)

    partner = device(x, y, z, 1 - c)

    def remote(src, dst, s, r, to):
        return pltpu.make_async_remote_copy(
            src_ref=src, dst_ref=dst, send_sem=s, recv_sem=r, device_id=to, device_id_type=MESH
        )

    context_in = pltpu.make_async_copy(context, cbuf.at[pl.ds(0, rows)], cin_sem)
    context_in.start()
    target_in = []
    stale_in = []
    for j in range(CHUNKS):
        part = pl.ds(j * cols, cols)
        target_in.append(
            pltpu.make_async_copy(target.at[:, part], tbuf.at[j, pl.ds(0, rows)], tin_sem.at[j])
        )
        stale_in.append(pltpu.make_async_copy(stale.at[0, :, part], sbuf.at[j], sin_sem.at[j]))
        target_in[j].start()
        stale_in[j].start()

    barrier = pltpu.get_barrier_semaphore()
    greeted = [partner]
    greeted += [x_peer(k) for k in range(1, NX)]
    greeted += [y_peer(k) for k in range(1, NY)]
    greeted += [z_peer(k) for k in range(1, NZ)]
    for to in greeted:
        pl.semaphore_signal(barrier, inc=1, device_id=to, device_id_type=MESH)

    group = 2 * NY * NZ * PIECE
    place = lax.broadcasted_iota(jnp.int32, (group, group), 0)
    natural = lax.broadcasted_iota(jnp.int32, (group, group), 1)

    def natural_of(i):
        ic, iy, iz, ir = i // 128, (i // 32) % 4, (i // 4) % 8, i % 4
        return (iz % 4) * 64 + ic * 32 + (iz // 4) * 16 + iy * 4 + ir

    perm[...] = jnp.where(natural == natural_of(place), 1.0, 0.0).astype(BF16)
    perm_t[...] = jnp.where(place == natural_of(natural), 1.0, 0.0).astype(BF16)
    tail = padded - rows
    cbuf[pl.ds(rows, tail)] = jnp.zeros((tail, width), BF16)
    ebuf[...] = jnp.zeros((padded, cols), BF16)
    for j in range(CHUNKS):
        tbuf[j, pl.ds(rows, tail)] = jnp.zeros((tail, cols), BF16)
    sqacc[...] = jnp.zeros(sqacc.shape, F32)

    pl.semaphore_wait(barrier, len(greeted))

    gz = []
    for k in range(1, NZ):
        gz.append(remote(weight, wz.at[z], gz_s.at[k - 1], gz_r.at[k - 1], z_peer(k)))
        gz[-1].start()
    wz[z] = weight[...]
    context_in.wait()

    def turn(m, carry):
        span = pl.ds(pl.multiple_of(m * 128, 128), 128)
        ct[:, span] = cbuf[span, :].T
        return carry

    blocks = padded // 128
    lax.fori_loop(0, 6, turn, 0)
    for copy in gz:
        copy.wait_recv()
    for i in range(NZ):
        wz32[pl.ds(i * PIECE, PIECE), :] = wz[i]
    own = wz32[...].astype(BF16)
    gb = []
    for j in range(CHUNKS):
        wbuf[j, c, am, bm] = own[:, j * cols : (j + 1) * cols]
    for j in range(CHUNKS):
        row = []
        for k in range(1, 4):
            at = wbuf.at[j, c, am, bm]
            i = j * 3 + k - 1
            row.append(remote(at, at, gb_s.at[i], gb_r.at[i], b_peer(lax.rem(bm + k, 4))))
            row[-1].start()
        gb.append(row)
    ga = []
    for j in range(CHUNKS):
        for copy in gb[j]:
            copy.wait_recv()
        row = []
        for k in range(1, 4):
            at = wbuf.at[j, c, am]
            i = j * 3 + k - 1
            row.append(remote(at, at, ga_s.at[i], ga_r.at[i], a_peer(lax.rem(am + k, 4))))
            row[-1].start()
        ga.append(row)
    lax.fori_loop(6, blocks, turn, 0)

    gd = []

    def to_partner(j):
        for copy in ga[j]:
            copy.wait_recv()
        at = wbuf.at[j, c]
        gd.append(remote(at, at, gd_s.at[j], gd_r.at[j], partner))
        gd[-1].start()

    span = width // 16
    scale = 1.0 / rows

    def compute(j):
        for g in range(NX):
            parts = [wbuf[j, 0, g, b] for b in range(4)] + [wbuf[j, 1, b, g] for b in range(4)]
            wn[pl.ds(g * group, group)] = jnp.dot(
                perm_t[...], jnp.concatenate(parts, axis=0), preferred_element_type=F32
            ).astype(BF16)
        tile = padded // 4

        def forward(m, carry):
            at = pl.ds(pl.multiple_of(m * tile, 16), tile)
            out = jnp.dot(cbuf[at, :], wn[...], preferred_element_type=F32)
            ebuf[at, :] = (out - tbuf[j, at].astype(F32)).astype(BF16)
            return carry

        lax.fori_loop(0, 4, forward, 0)

        def backward(g, carry):
            at = pl.ds(pl.multiple_of(g * group, group), group)
            grad = jnp.dot(ct[at, :], ebuf[...], preferred_element_type=F32) * scale
            old = sbuf[j, at].astype(F32)
            chosen = []
            fresh = []
            for i in range(group // span):
                b = g * (group // span) + i
                flag = trigger[0, b].astype(F32)
                mine = grad[i * span : (i + 1) * span]
                past = old[i * span : (i + 1) * span]
                diff = mine - past
                sq = (diff * diff).reshape(span // 8, 8, cols).sum(axis=0)
                sqacc[b] = sqacc[b] + sq[:, : cols // 2] + sq[:, cols // 2 :]
                chosen.append((diff * flag).astype(BF16))
                fresh.append((flag * mine + (1.0 - flag) * past).astype(BF16))
            fbuf[j, at] = jnp.concatenate(fresh, axis=0)
            moved = jnp.dot(
                perm[...], jnp.concatenate(chosen, axis=0), preferred_element_type=F32
            ).astype(BF16)
            for b in range(4):
                half[j, 0, g, b] = moved[b * 32 : (b + 1) * 32]
                half[j, 1, b, g] = moved[128 + b * 32 : 128 + (b + 1) * 32]
            return carry

        lax.fori_loop(0, NX, backward, 0)

    rd, ra, rb, rz, fout = [], [], [], [], []

    def send_d(j):
        rd.append(remote(half.at[j, 1 - c], drecv.at[j], rd_s.at[j], rd_r.at[j], partner))
        rd[-1].start()
        fout.append(
            pltpu.make_async_copy(
                fbuf.at[j], stale_out.at[0, :, pl.ds(j * cols, cols)], fout_sem.at[j]
            )
        )
        fout[-1].start()

    def send_a(j):
        rd[j].wait_recv()
        asend[j] = (half[j, c].astype(F32) + drecv[j].astype(F32)).astype(BF16)
        row = []
        for k in range(1, 4):
            a = lax.rem(am + k, 4)
            i = j * 3 + k - 1
            row.append(
                remote(asend.at[j, a], arecv.at[j, k - 1], ra_s.at[i], ra_r.at[i], a_peer(a))
            )
            row[-1].start()
        ra.append(row)

    def send_b(j):
        for copy in ra[j]:
            copy.wait_recv()
        total = asend[j, am].astype(F32)
        for k in range(3):
            total = total + arecv[j, k].astype(F32)
        bsend[j] = total.astype(BF16)
        row = []
        for k in range(1, 4):
            b = lax.rem(bm + k, 4)
            i = j * 3 + k - 1
            row.append(
                remote(bsend.at[j, b], brecv.at[j, k - 1], rb_s.at[i], rb_r.at[i], b_peer(b))
            )
            row[-1].start()
        rb.append(row)

    def send_z(j):
        for copy in rb[j]:
            copy.wait_recv()
        total = bsend[j, bm].astype(F32)
        for k in range(3):
            total = total + brecv[j, k].astype(F32)
        for i in range(NZ):
            zsend[j, i] = total[i * PIECE : (i + 1) * PIECE]
        row = []
        for k in range(1, NZ):
            i = j * 7 + k - 1
            row.append(
                remote(
                    zsend.at[j, lax.rem(z + k, NZ)],
                    zrecv.at[j, k - 1],
                    rz_s.at[i],
                    rz_r.at[i],
                    z_peer(k),
                )
            )
            row[-1].start()
        rz.append(row)

    to_partner(0)
    for j in range(CHUNKS):
        if j + 1 < CHUNKS:
            to_partner(j + 1)
        gd[j].wait_recv()
        target_in[j].wait()
        stale_in[j].wait()
        compute(j)
        send_d(j)
        if j >= 1:
            send_a(j - 1)
        if j >= 2:
            send_b(j - 2)
        if j >= 3:
            send_z(j - 3)

    def spread(src, bufs, at, peers, first):
        out = []
        for k, to in enumerate(peers):
            out.append(remote(src, bufs.at[at], n_s.at[first + k], n_r.at[first + k], to))
            out[-1].start()
        return out

    nrm[0] = sqacc[...].sum(axis=1)
    sent = spread(nrm.at[0], nrm, 1, [partner], 0)
    last = CHUNKS - 1
    send_a(last)
    sent[0].wait_recv()
    nx_buf[x] = nrm[0] + nrm[1]
    sent_x = spread(nx_buf.at[x], nx_buf, x, [x_peer(k) for k in range(1, NX)], 1)
    send_b(last - 1)
    send_z(last - 2)
    send_b(last)
    for copy in sent_x:
        copy.wait_recv()
    ny_buf[y] = (nx_buf[0] + nx_buf[1]) + (nx_buf[2] + nx_buf[3])
    sent_y = spread(ny_buf.at[y], ny_buf, y, [y_peer(k) for k in range(1, NY)], 4)
    send_z(last - 1)
    send_z(last)
    for copy in sent_y:
        copy.wait_recv()
    nz_buf[z] = (ny_buf[0] + ny_buf[1]) + (ny_buf[2] + ny_buf[3])
    sent_z = spread(nz_buf.at[z], nz_buf, z, [z_peer(k) for k in range(1, NZ)], 7)

    for j in range(CHUNKS):
        for copy in rz[j]:
            copy.wait_recv()
        total = zsend[j, z]
        for k in range(NZ - 1):
            total = total + zrecv[j, k]
        summed_out[:, pl.ds(j * cols, cols)] = total
    for copy in sent_z:
        copy.wait_recv()
    every = nz_buf[0]
    for i in range(1, NZ):
        every = every + nz_buf[i]
    norms_out[...] = jnp.broadcast_to(jnp.sum(every, axis=1, keepdims=True), norms_out.shape)

    for copy in gz + gd + rd + sent + sent_x + sent_y + sent_z:
        copy.wait_send()
    for rows_of in (gb, ga, ra, rb, rz):
        for row in rows_of:
            for copy in row:
                copy.wait_send()
    for copy in fout:
        copy.wait()


def step(context, target, weight, stale, trigger):
    rows, width = context.shape
    cols = width // CHUNKS
    padded = -(-rows // 128) * 128
    dma = pltpu.SemaphoreType.DMA
    half = width // 2
    vmem = pl.BlockSpec(memory_space=pltpu.VMEM)
    hbm = pl.BlockSpec(memory_space=pl.ANY)
    return pl.pallas_call(
        functools.partial(step_kernel, rows, padded),
        out_shape=(
            jax.ShapeDtypeStruct((PIECE, width), F32),
            jax.ShapeDtypeStruct((1, width, width), BF16),
            jax.ShapeDtypeStruct((16, 128), F32),
        ),
        in_specs=[hbm, hbm, vmem, hbm, pl.BlockSpec(memory_space=pltpu.SMEM)],
        out_specs=(vmem, hbm, vmem),
        scratch_shapes=[
            pltpu.VMEM((padded, width), BF16),
            pltpu.VMEM((width, padded), BF16),
            pltpu.VMEM((CHUNKS, padded, cols), BF16),
            pltpu.VMEM((CHUNKS, width, cols), BF16),
            pltpu.VMEM((CHUNKS, width, cols), BF16),
            pltpu.VMEM((256, 256), BF16),
            pltpu.VMEM((256, 256), BF16),
            pltpu.VMEM((NZ, PIECE, width), F32),
            pltpu.VMEM((NZ * PIECE, width), F32),
            pltpu.VMEM((CHUNKS, 2, 4, 4, 32, cols), BF16),
            pltpu.VMEM((width, cols), BF16),
            pltpu.VMEM((padded, cols), BF16),
            pltpu.VMEM((CHUNKS, 2, 4, 4, 32, cols), BF16),
            pltpu.VMEM((CHUNKS, 4, 4, 32, cols), BF16),
            pltpu.VMEM((CHUNKS, 4, 4, 32, cols), BF16),
            pltpu.VMEM((CHUNKS, 3, 4, 32, cols), BF16),
            pltpu.VMEM((CHUNKS, 4, 32, cols), BF16),
            pltpu.VMEM((CHUNKS, 3, 32, cols), BF16),
            pltpu.VMEM((CHUNKS, NZ, PIECE, cols), F32),
            pltpu.VMEM((CHUNKS, NZ - 1, PIECE, cols), F32),
            pltpu.VMEM((16, 8, 128), F32),
            pltpu.VMEM((2, 16, 128), F32),
            pltpu.VMEM((NX, 16, 128), F32),
            pltpu.VMEM((NY, 16, 128), F32),
            pltpu.VMEM((NZ, 16, 128), F32),
            dma,
            dma((CHUNKS,)),
            dma((CHUNKS,)),
            dma((CHUNKS,)),
            dma((NZ - 1,)),
            dma((NZ - 1,)),
            dma((CHUNKS * 3,)),
            dma((CHUNKS * 3,)),
            dma((CHUNKS * 3,)),
            dma((CHUNKS * 3,)),
            dma((CHUNKS,)),
            dma((CHUNKS,)),
            dma((CHUNKS,)),
            dma((CHUNKS,)),
            dma((CHUNKS * 3,)),
            dma((CHUNKS * 3,)),
            dma((CHUNKS * 3,)),
            dma((CHUNKS * 3,)),
            dma((CHUNKS * 7,)),
            dma((CHUNKS * 7,)),
            dma((14,)),
            dma((14,)),
        ],
        compiler_params=pltpu.CompilerParams(
            collective_id=0, has_side_effects=True, vmem_limit_bytes=60 * 1024 * 1024
        ),
        name="step",
    )(context, target, weight, stale, trigger)


def body(context, target, weight, stale, trigger, aggregate, moment, second):
    summed, stale_new, norms = step(context, target, weight, stale, trigger)
    aggregate_new = aggregate + summed
    moment_new = 0.9 * moment + 0.1 * aggregate_new
    second_new = 0.999 * second + 0.001 * aggregate_new * aggregate_new
    weight_new = weight - 0.001 * (moment_new / (jnp.sqrt(second_new) + 1e-08) + 0.05 * weight)
    return (aggregate_new, weight_new, moment_new, second_new, stale_new, norms[:, 0])


def solution(mesh):
    split = P(("dp", "sub"), None)
    return jax.shard_map(
        body,
        mesh=mesh,
        in_specs=(split, split, split, P(("dp", "sub"), None, None), split, split, split, split),
        out_specs=(split, split, split, split, P(("dp", "sub"), None, None), P()),
        check_vma=False,
    )
```

time: 232 us -> 69.1 us (0.30)
  blocking collectives: 123 us -> 0 us
  Pallas kernels: 0 us -> 62 us
  waiting for transfers between devices: 54.6 us -> 0 us
  matrix products: 14.1 us -> 0 us
  between operations: 14.1 us -> 0.68 us
  other arithmetic: 11.8 us -> 1.37 us
  starting transfers between devices: 6.18 us -> 0 us
  local copies, waits for them, and re-layouts: 8 us -> 4.42 us
    all_to_all x2 -> x0, blocking collectives: 79.1 us -> none  [the longest x1 58.8 us: sent_and_summed(): lax.all_to_all(pieces, axis, split_axis=0, concat_axis=0, tiled=True)]
    pallas_call x0 -> x1, Pallas kernels: none -> 62 us  [step(): pl.pallas_call(functools.partial(step_kernel, rows, padded), out_shape=(j...]
    all_gather x1 -> x0, waiting for transfers between devices: 54.6 us -> none  [body(): low_whole = lax.all_gather(low_group, DP, axis=0, tiled=True)]
    psum x5 -> x0, blocking collectives: 43.7 us -> none  [one_axis_at_a_time(): return functools.reduce(lax.psum, axes, value)]
    dot_general x1 -> x0, matrix products: 14.1 us -> none  [body(): lax.dot_general(context, error, (((0,), (0,)), ((), ())), preferred_eleme...]
    all_to_all x1 -> x0, starting transfers between devices: 6.14 us -> none  [sent_and_summed(): lax.all_to_all(pieces, axis, split_axis=0, concat_axis=0, tiled=True)]
    reshape x2 -> x0, local copies, waits for them, and re-layouts: 5.81 us -> none  [the longest x1 5.17 us: body(): blocked = (grad - old).reshape(blocks, span, width)]
    transpose x1 -> x0, other arithmetic: 4.68 us -> none  [in_blocks(): return jnp.moveaxis(pieces, dim, 0)]
  transfers between devices with their start and end apart: 2 -> 0, of which waited for: 1 -> 0; matrix products, arithmetic and copies ran while one was open for 1% -> 0% of each run, Pallas kernels for 0% -> 0%
where the time goes in v1:
time: 69.1 us; the launch traced here: 68.5 us
  Pallas kernels  62 us (90%)
  local copies, waits for them, and re-layouts  4.42 us (6%)
  other arithmetic  1.37 us (2%)
    pallas_call x1, Pallas kernels, step(): pl.pallas_call(functools.partial(step_kernel, rows, padded), out_shape=(j...  62 us
    unnamed x9, local copies, waits for them, and re-layouts  3.1 us

profile of v1, /device:TPU:8, one launch (start us, length us, event | category | flops | bytes accessed | tf_op | source)
XLA Modules:
  0.0 68.5 jit_solution(2965012985575902197)
XLA Ops:
  0.6 0.0 copy-start
  0.6 0.0 copy-start.1
  0.7 0.0 copy-start.2
  0.7 0.0 copy-start.3
  0.7 62.0 %step.1 = (f32[4,1024]{1,0:T(4,128)}, bf16[1,1024,1024]{2,1,0:T(8,128)(2,1)}, f32[16,128]{1,0:T(8,128)}) custom-call(bf16[1576,1024]{1,0:T(8,128)(2,1)} %context.1, bf16[1576,1024]{1,0:T(8,128)(2,1)} %target.1, f32[4,1024]{1,0:T(4,128)} %weight.1, bf16[1,1024,1024]{2,1,0:T(8,128)(2,1)} %stale.1, s32[1,16]{1,0:T(1,128)} %trigger.1), custom_call_target="tpu_custom_call" | custom-call | tf_op jit(solution)/shard_map/step/pallas_call | solution.py:396
  62.7 1.3 %slice_reduce_fusion = f32[16]{0:T(128)} fusion(f32[16,128]{1,0:T(8,128)} %get-tuple-element.11), kind=kLoop, calls=%fused_computation.4 | loop fusion | bytes 128 | tf_op jit(solution)/shard_map/slice | solution.py:467
  64.0 0.0 copy-done
  64.0 0.0 copy-done.1
  64.0 0.0 copy-done.2
  64.0 0.0 copy-done.3
  64.0 1.4 %multiply_subtract_fusion = (f32[4,1024]{1,0:T(4,128)}, f32[4,1024]{1,0:T(4,128)}, f32[4,1024]{1,0:T(4,128)}, f32[4,1024]{1,0:T(4,128)}) fusion(f32[4,1024]{1,0:T(4,128)S(1)} %copy-done, f32[4,1024]{1,0:T(4,128)S(1)} %copy-done.1, f32[4,1024]{1,0:T(4,128)S(1)} %copy-done.2, f32[4,1024]{1,0:T(4,128)S(1)} %copy-done.3, f32[4,1024]{1,0:T(4,128)} %get-tuple-element.9), kind=kLoop, calls=%fused_computation.2 | loop fusion | flops 57344 | bytes 147456 | tf_op jit(solution)/shard_map/sub | solution.py:466
  65.4 3.1 %copy.15 = bf16[1,1024,1024]{2,1,0:T(8,128)(2,1)} copy(bf16[1,1024,1024]{2,1,0:T(8,128)(2,1)} %get-tuple-element.26) | data formatting | bytes 4194304
Async XLA Ops:
  0.6 63.4 %copy-start = (f32[4,1024]{1,0:T(4,128)S(1)}, f32[4,1024]{1,0:T(4,128)}, u32[]{:S(2)}) copy-start(f32[4,1024]{1,0:T(4,128)} %weight.1) | copy-start | bytes 49156
  0.6 63.4 %copy-start.1 = (f32[4,1024]{1,0:T(4,128)S(1)}, f32[4,1024]{1,0:T(4,128)}, u32[]{:S(2)}) copy-start(f32[4,1024]{1,0:T(4,128)} %param.15) | copy-start | bytes 49156
  0.7 63.4 %copy-start.2 = (f32[4,1024]{1,0:T(4,128)S(1)}, f32[4,1024]{1,0:T(4,128)}, u32[]{:S(2)}) copy-start(f32[4,1024]{1,0:T(4,128)} %param.14) | copy-start | bytes 49156
  0.7 63.3 %copy-start.3 = (f32[4,1024]{1,0:T(4,128)S(1)}, f32[4,1024]{1,0:T(4,128)}, u32[]{:S(2)}) copy-start(f32[4,1024]{1,0:T(4,128)} %param.13) | copy-start | bytes 49156

commit v2 on v1

--- a/solution.py
+++ b/solution.py
@@ -38,7 +38,7 @@
     wz,
     wz32,
     wbuf,
-    wn,
+    own_low,
     ebuf,
     half,
     drecv,
@@ -49,6 +49,7 @@
     zsend,
     zrecv,
     sqacc,
+    flags,
     nrm,
     nx_buf,
     ny_buf,
@@ -56,7 +57,6 @@
     cin_sem,
     tin_sem,
     sin_sem,
-    fout_sem,
     gz_s,
     gz_r,
     gb_s,
@@ -145,6 +145,7 @@
 
     perm[...] = jnp.where(natural == natural_of(place), 1.0, 0.0).astype(BF16)
     perm_t[...] = jnp.where(place == natural_of(natural), 1.0, 0.0).astype(BF16)
+    own_low[...] = weight[...].astype(BF16)
     tail = padded - rows
     cbuf[pl.ds(rows, tail)] = jnp.zeros((tail, width), BF16)
     ebuf[...] = jnp.zeros((padded, cols), BF16)
@@ -156,22 +157,25 @@
 
     gz = []
     for k in range(1, NZ):
-        gz.append(remote(weight, wz.at[z], gz_s.at[k - 1], gz_r.at[k - 1], z_peer(k)))
+        gz.append(remote(own_low, wz.at[z], gz_s.at[k - 1], gz_r.at[k - 1], z_peer(k)))
         gz[-1].start()
-    wz[z] = weight[...]
+    wz[z] = own_low[...]
     context_in.wait()
 
     def turn(m, carry):
         span = pl.ds(pl.multiple_of(m * 128, 128), 128)
-        ct[:, span] = cbuf[span, :].T
+        for g in range(NX):
+            at = pl.ds(g * group, group)
+            moved = jnp.dot(cbuf[span, at], perm_t[...], preferred_element_type=F32).astype(BF16)
+            cbuf[span, at] = moved
+            ct[at, span] = moved.T
         return carry
 
-    blocks = padded // 128
-    lax.fori_loop(0, 6, turn, 0)
+    lax.fori_loop(0, padded // 128, turn, 0)
     for copy in gz:
         copy.wait_recv()
     for i in range(NZ):
-        wz32[pl.ds(i * PIECE, PIECE), :] = wz[i]
+        wz32[pl.ds(i * PIECE, PIECE), :] = wz[i].astype(F32)
     own = wz32[...].astype(BF16)
     gb = []
     for j in range(CHUNKS):
@@ -195,7 +199,17 @@
             row.append(remote(at, at, ga_s.at[i], ga_r.at[i], a_peer(lax.rem(am + k, 4))))
             row[-1].start()
         ga.append(row)
-    lax.fori_loop(6, blocks, turn, 0)
+    for j in range(CHUNKS):
+        stale_in[j].wait()
+        for g in range(NX):
+            at = pl.ds(g * group, group)
+            sbuf[j, at] = jnp.dot(perm[...], sbuf[j, at], preferred_element_type=F32).astype(BF16)
+    low = lax.broadcasted_iota(jnp.int32, (16, cols), 0) // PIECE
+    for g in range(NX):
+        flag = jnp.zeros((16, cols), F32)
+        for i in range(4):
+            flag = jnp.where(low == i, trigger[0, g * 4 + i].astype(F32), flag)
+        flags[g] = flag
 
     gd = []
 
@@ -206,63 +220,48 @@
         gd.append(remote(at, at, gd_s.at[j], gd_r.at[j], partner))
         gd[-1].start()
 
-    span = width // 16
     scale = 1.0 / rows
-
-    def compute(j):
+    tile = padded // 4
+
+    def forward(j):
+        parts = []
         for g in range(NX):
-            parts = [wbuf[j, 0, g, b] for b in range(4)] + [wbuf[j, 1, b, g] for b in range(4)]
-            wn[pl.ds(g * group, group)] = jnp.dot(
-                perm_t[...], jnp.concatenate(parts, axis=0), preferred_element_type=F32
+            parts += [wbuf[j, 0, g, b] for b in range(4)] + [wbuf[j, 1, b, g] for b in range(4)]
+        low_part = jnp.concatenate(parts, axis=0)
+        for m in range(4):
+            at = pl.ds(m * tile, tile)
+            out = jnp.dot(cbuf[at, :], low_part, preferred_element_type=F32)
+            ebuf[at, :] = (out - tbuf[j, at].astype(F32)).astype(BF16)
+
+    def backward(j):
+        for g in range(NX):
+            at = pl.ds(g * group, group)
+            grad = jnp.dot(ct[at, :], ebuf[...], preferred_element_type=F32) * scale
+            mine = grad.reshape(16, 16, cols)
+            past = sbuf[j, at].astype(F32).reshape(16, 16, cols)
+            flag = flags[g][None]
+            diff = mine - past
+            sq = (diff * diff).sum(axis=0)
+            sqacc[g] = sqacc[g] + sq[:, : cols // 2] + sq[:, cols // 2 :]
+            chosen = (diff * flag).reshape(group, cols).astype(BF16)
+            fresh = flag * mine + (1.0 - flag) * past
+            fbuf[j, at] = fresh.reshape(group, cols).astype(BF16)
+            for b in range(4):
+                half[j, 0, g, b] = chosen[b * 32 : (b + 1) * 32]
+                half[j, 1, b, g] = chosen[128 + b * 32 : 128 + (b + 1) * 32]
+
+    def finish(j):
+        for g in range(NX):
+            at = pl.ds(g * group, group)
+            stale_out[0, at, pl.ds(j * cols, cols)] = jnp.dot(
+                perm_t[...], fbuf[j, at], preferred_element_type=F32
             ).astype(BF16)
-        tile = padded // 4
-
-        def forward(m, carry):
-            at = pl.ds(pl.multiple_of(m * tile, 16), tile)
-            out = jnp.dot(cbuf[at, :], wn[...], preferred_element_type=F32)
-            ebuf[at, :] = (out - tbuf[j, at].astype(F32)).astype(BF16)
-            return carry
-
-        lax.fori_loop(0, 4, forward, 0)
-
-        def backward(g, carry):
-            at = pl.ds(pl.multiple_of(g * group, group), group)
-            grad = jnp.dot(ct[at, :], ebuf[...], preferred_element_type=F32) * scale
-            old = sbuf[j, at].astype(F32)
-            chosen = []
-            fresh = []
-            for i in range(group // span):
-                b = g * (group // span) + i
-                flag = trigger[0, b].astype(F32)
-                mine = grad[i * span : (i + 1) * span]
-                past = old[i * span : (i + 1) * span]
-                diff = mine - past
-                sq = (diff * diff).reshape(span // 8, 8, cols).sum(axis=0)
-                sqacc[b] = sqacc[b] + sq[:, : cols // 2] + sq[:, cols // 2 :]
-                chosen.append((diff * flag).astype(BF16))
-                fresh.append((flag * mine + (1.0 - flag) * past).astype(BF16))
-            fbuf[j, at] = jnp.concatenate(fresh, axis=0)
-            moved = jnp.dot(
-                perm[...], jnp.concatenate(chosen, axis=0), preferred_element_type=F32
-            ).astype(BF16)
-            for b in range(4):
-                half[j, 0, g, b] = moved[b * 32 : (b + 1) * 32]
-                half[j, 1, b, g] = moved[128 + b * 32 : 128 + (b + 1) * 32]
-            return carry
-
-        lax.fori_loop(0, NX, backward, 0)
-
-    rd, ra, rb, rz, fout = [], [], [], [], []
+
+    rd, ra, rb, rz = [], [], [], []
 
     def send_d(j):
         rd.append(remote(half.at[j, 1 - c], drecv.at[j], rd_s.at[j], rd_r.at[j], partner))
         rd[-1].start()
-        fout.append(
-            pltpu.make_async_copy(
-                fbuf.at[j], stale_out.at[0, :, pl.ds(j * cols, cols)], fout_sem.at[j]
-            )
-        )
-        fout[-1].start()
 
     def send_a(j):
         rd[j].wait_recv()
@@ -301,7 +300,7 @@
         for k in range(3):
             total = total + brecv[j, k].astype(F32)
         for i in range(NZ):
-            zsend[j, i] = total[i * PIECE : (i + 1) * PIECE]
+            zsend[j, i] = total[i * PIECE : (i + 1) * PIECE].astype(BF16)
         row = []
         for k in range(1, NZ):
             i = j * 7 + k - 1
@@ -319,19 +318,17 @@
 
     to_partner(0)
     for j in range(CHUNKS):
+        gd[j].wait_recv()
+        target_in[j].wait()
+        forward(j)
         if j + 1 < CHUNKS:
             to_partner(j + 1)
-        gd[j].wait_recv()
-        target_in[j].wait()
-        stale_in[j].wait()
-        compute(j)
-        send_d(j)
         if j >= 1:
             send_a(j - 1)
-        if j >= 2:
-            send_b(j - 2)
         if j >= 3:
-            send_z(j - 3)
+            send_b(j - 3)
+        backward(j)
+        send_d(j)
 
     def spread(src, bufs, at, peers, first):
         out = []
@@ -340,22 +337,34 @@
             out[-1].start()
         return out
 
-    nrm[0] = sqacc[...].sum(axis=1)
+    pick = lax.broadcasted_iota(jnp.int32, (16, 64), 1) // PIECE
+    pick = jnp.where(pick == lax.broadcasted_iota(jnp.int32, (16, 64), 0), 1.0, 0.0)
+    nrm[0] = jnp.dot(
+        pick.astype(F32),
+        sqacc[...].reshape(64, 128),
+        precision=lax.Precision.HIGHEST,
+        preferred_element_type=F32,
+    )
     sent = spread(nrm.at[0], nrm, 1, [partner], 0)
-    last = CHUNKS - 1
-    send_a(last)
+    send_b(1)
+    send_z(0)
+    send_a(3)
     sent[0].wait_recv()
     nx_buf[x] = nrm[0] + nrm[1]
     sent_x = spread(nx_buf.at[x], nx_buf, x, [x_peer(k) for k in range(1, NX)], 1)
-    send_b(last - 1)
-    send_z(last - 2)
-    send_b(last)
+    send_z(1)
+    finish(0)
+    finish(1)
+    send_b(2)
+    finish(2)
+    finish(3)
+    send_b(3)
     for copy in sent_x:
         copy.wait_recv()
     ny_buf[y] = (nx_buf[0] + nx_buf[1]) + (nx_buf[2] + nx_buf[3])
     sent_y = spread(ny_buf.at[y], ny_buf, y, [y_peer(k) for k in range(1, NY)], 4)
-    send_z(last - 1)
-    send_z(last)
+    send_z(2)
+    send_z(3)
     for copy in sent_y:
         copy.wait_recv()
     nz_buf[z] = (ny_buf[0] + ny_buf[1]) + (ny_buf[2] + ny_buf[3])
@@ -364,16 +373,19 @@
     for j in range(CHUNKS):
         for copy in rz[j]:
             copy.wait_recv()
-        total = zsend[j, z]
+        total = zsend[j, z].astype(F32)
         for k in range(NZ - 1):
-            total = total + zrecv[j, k]
+            total = total + zrecv[j, k].astype(F32)
         summed_out[:, pl.ds(j * cols, cols)] = total
     for copy in sent_z:
         copy.wait_recv()
     every = nz_buf[0]
     for i in range(1, NZ):
         every = every + nz_buf[i]
-    norms_out[...] = jnp.broadcast_to(jnp.sum(every, axis=1, keepdims=True), norms_out.shape)
+    sums = jnp.broadcast_to(jnp.sum(every, axis=1, keepdims=True), (16, 128))
+    row = lax.broadcasted_iota(jnp.int32, (16, 128), 0)
+    lane = lax.broadcasted_iota(jnp.int32, (16, 128), 1)
+    norms_out[...] = jnp.sum(jnp.where(row == lane, sums, 0.0), axis=0, keepdims=True)
 
     for copy in gz + gd + rd + sent + sent_x + sent_y + sent_z:
         copy.wait_send()
@@ -381,8 +393,6 @@
         for row in rows_of:
             for copy in row:
                 copy.wait_send()
-    for copy in fout:
-        copy.wait()
 
 
 def step(context, target, weight, stale, trigger):
@@ -390,18 +400,17 @@
     cols = width // CHUNKS
     padded = -(-rows // 128) * 128
     dma = pltpu.SemaphoreType.DMA
-    half = width // 2
     vmem = pl.BlockSpec(memory_space=pltpu.VMEM)
-    hbm = pl.BlockSpec(memory_space=pl.ANY)
+    hbm = pl.BlockSpec(memory_space=pltpu.HBM)
     return pl.pallas_call(
         functools.partial(step_kernel, rows, padded),
         out_shape=(
             jax.ShapeDtypeStruct((PIECE, width), F32),
             jax.ShapeDtypeStruct((1, width, width), BF16),
-            jax.ShapeDtypeStruct((16, 128), F32),
+            jax.ShapeDtypeStruct((1, 128), F32),
         ),
         in_specs=[hbm, hbm, vmem, hbm, pl.BlockSpec(memory_space=pltpu.SMEM)],
-        out_specs=(vmem, hbm, vmem),
+        out_specs=(vmem, vmem, vmem),
         scratch_shapes=[
             pltpu.VMEM((padded, width), BF16),
             pltpu.VMEM((width, padded), BF16),
@@ -410,10 +419,10 @@
             pltpu.VMEM((CHUNKS, width, cols), BF16),
             pltpu.VMEM((256, 256), BF16),
             pltpu.VMEM((256, 256), BF16),
-            pltpu.VMEM((NZ, PIECE, width), F32),
+            pltpu.VMEM((NZ, PIECE, width), BF16),
             pltpu.VMEM((NZ * PIECE, width), F32),
             pltpu.VMEM((CHUNKS, 2, 4, 4, 32, cols), BF16),
-            pltpu.VMEM((width, cols), BF16),
+            pltpu.VMEM((PIECE, width), BF16),
             pltpu.VMEM((padded, cols), BF16),
             pltpu.VMEM((CHUNKS, 2, 4, 4, 32, cols), BF16),
             pltpu.VMEM((CHUNKS, 4, 4, 32, cols), BF16),
@@ -421,15 +430,15 @@
             pltpu.VMEM((CHUNKS, 3, 4, 32, cols), BF16),
             pltpu.VMEM((CHUNKS, 4, 32, cols), BF16),
             pltpu.VMEM((CHUNKS, 3, 32, cols), BF16),
-            pltpu.VMEM((CHUNKS, NZ, PIECE, cols), F32),
-            pltpu.VMEM((CHUNKS, NZ - 1, PIECE, cols), F32),
-            pltpu.VMEM((16, 8, 128), F32),
+            pltpu.VMEM((CHUNKS, NZ, PIECE, cols), BF16),
+            pltpu.VMEM((CHUNKS, NZ - 1, PIECE, cols), BF16),
+            pltpu.VMEM((4, 16, 128), F32),
+            pltpu.VMEM((4, 16, cols), F32),
             pltpu.VMEM((2, 16, 128), F32),
             pltpu.VMEM((NX, 16, 128), F32),
             pltpu.VMEM((NY, 16, 128), F32),
             pltpu.VMEM((NZ, 16, 128), F32),
             dma,
-            dma((CHUNKS,)),
             dma((CHUNKS,)),
             dma((CHUNKS,)),
             dma((NZ - 1,)),
@@ -452,7 +461,7 @@
             dma((14,)),
         ],
         compiler_params=pltpu.CompilerParams(
-            collective_id=0, has_side_effects=True, vmem_limit_bytes=60 * 1024 * 1024
+            collective_id=0, has_side_effects=True, vmem_limit_bytes=50 * 1024 * 1024
         ),
         name="step",
     )(context, target, weight, stale, trigger)
@@ -464,7 +473,7 @@
     moment_new = 0.9 * moment + 0.1 * aggregate_new
     second_new = 0.999 * second + 0.001 * aggregate_new * aggregate_new
     weight_new = weight - 0.001 * (moment_new / (jnp.sqrt(second_new) + 1e-08) + 0.05 * weight)
-    return (aggregate_new, weight_new, moment_new, second_new, stale_new, norms[:, 0])
+    return (aggregate_new, weight_new, moment_new, second_new, stale_new, norms[0, :16])
 
 
 def solution(mesh):

time: 69.1 us -> 58.1 us (0.84)
  Pallas kernels: 62 us -> 53.3 us
  local copies, waits for them, and re-layouts: 4.42 us -> 3.21 us
  other arithmetic: 1.37 us -> 0.65 us
    pallas_call x1, Pallas kernels: 62 us -> 53.3 us  [step(): pl.pallas_call(functools.partial(step_kernel, rows, padded), out_shape=(j...]
    slice x1 -> x0, local copies, waits for them, and re-layouts: 1.32 us -> none  [body(): norms[:, 0]]
    sub x1, other arithmetic: 1.37 us -> 0.65 us  [body(): weight - 0.001 * (moment_new / (jnp.sqrt(second_new) + 1e-08) + 0.05 * we...]
    unnamed x9 -> x11, local copies, waits for them, and re-layouts: 3.1 us -> 2.69 us
where the time goes in v2:
time: 58.1 us; the launch traced here: 57.8 us
  Pallas kernels  53.3 us (92%)
  local copies, waits for them, and re-layouts  3.21 us (6%)
  between operations  0.66 us (1%)
  other arithmetic  0.65 us (1%)
    pallas_call x1, Pallas kernels, step(): pl.pallas_call(functools.partial(step_kernel, rows, padded), out_shape=(j...  53.3 us
    unnamed x11, local copies, waits for them, and re-layouts  2.69 us

profile of v2, /device:TPU:8, one launch (start us, length us, event | category | flops | bytes accessed | tf_op | source)
XLA Modules:
  0.0 57.8 jit_solution(7043677473587873637)
XLA Ops:
  0.6 0.0 copy-start
  0.6 0.7 %copy-done = f32[4,1024]{1,0:T(4,128)S(1)} copy-done((f32[4,1024]{1,0:T(4,128)S(1)}, f32[4,1024]{1,0:T(4,128)}, u32[]{:S(2)}) %copy-start) | copy-done | bytes 16408
  1.4 0.0 copy-start.1
  1.4 0.7 %copy-done.1 = s32[1,16]{1,0:T(1,128)S(1)} copy-done((s32[1,16]{1,0:T(1,128)S(1)}, s32[1,16]{1,0:T(1,128)}, u32[]{:S(2)}) %copy-start.1) | copy-done | bytes 88
  2.0 0.0 copy-start.2
  2.0 0.0 copy-start.3
  2.0 0.0 copy-start.4
  2.0 53.3 %step.1 = (f32[4,1024]{1,0:T(4,128)S(1)}, bf16[1,1024,1024]{2,1,0:T(8,128)(2,1)S(1)}, f32[1,128]{1,0:T(1,128)S(1)}) custom-call(bf16[1576,1024]{1,0:T(8,128)(2,1)} %context.1, bf16[1576,1024]{1,0:T(8,128)(2,1)} %target.1, f32[4,1024]{1,0:T(4,128)S(1)} %copy-done, bf16[1,1024,1024]{2,1,0:T(8,128)(2,1)} %stale.1, s32[1,16]{1,0:T(1,128)S(1)} %copy-done.1), custom_call_target="tpu_custom_call" | custom-call | tf_op jit(solution)/shard_map/step/pallas_call | solution.py:405
  55.3 0.5 slice_bitcast_fusion
  55.8 0.0 copy-done.2
  55.9 0.0 copy-done.3
  55.9 0.0 copy-done.4
  55.9 0.7 %multiply_subtract_fusion = (f32[4,1024]{1,0:T(4,128)}, f32[4,1024]{1,0:T(4,128)}, f32[4,1024]{1,0:T(4,128)}, f32[4,1024]{1,0:T(4,128)}) fusion(f32[4,1024]{1,0:T(4,128)S(1)} %copy-done, f32[4,1024]{1,0:T(4,128)S(1)} %copy-done.2, f32[4,1024]{1,0:T(4,128)S(1)} %copy-done.3, f32[4,1024]{1,0:T(4,128)S(1)} %copy-done.4, f32[4,1024]{1,0:T(4,128)S(1)} %get-tuple-element.9), kind=kLoop, calls=%fused_computation.2 | loop fusion | flops 57344 | bytes 147456 | tf_op jit(solution)/shard_map/sub | solution.py:475
  56.5 1.3 %copy.15 = bf16[1,1024,1024]{2,1,0:T(8,128)(2,1)} copy(bf16[1,1024,1024]{2,1,0:T(8,128)(2,1)S(1)} %get-tuple-element.26) | data formatting | bytes 4194304
Async XLA Ops:
  0.6 0.7 %copy-start = (f32[4,1024]{1,0:T(4,128)S(1)}, f32[4,1024]{1,0:T(4,128)}, u32[]{:S(2)}) copy-start(f32[4,1024]{1,0:T(4,128)} %weight.1) | copy-start | bytes 49156
  1.4 0.7 %copy-start.1 = (s32[1,16]{1,0:T(1,128)S(1)}, s32[1,16]{1,0:T(1,128)}, u32[]{:S(2)}) copy-start(s32[1,16]{1,0:T(1,128)} %trigger.1) | copy-start | bytes 196
  2.0 53.8 %copy-start.2 = (f32[4,1024]{1,0:T(4,128)S(1)}, f32[4,1024]{1,0:T(4,128)}, u32[]{:S(2)}) copy-start(f32[4,1024]{1,0:T(4,128)} %param.15) | copy-start | bytes 49156
  2.0 53.8 %copy-start.3 = (f32[4,1024]{1,0:T(4,128)S(1)}, f32[4,1024]{1,0:T(4,128)}, u32[]{:S(2)}) copy-start(f32[4,1024]{1,0:T(4,128)} %param.14) | copy-start | bytes 49156
  2.0 53.8 %copy-start.4 = (f32[4,1024]{1,0:T(4,128)S(1)}, f32[4,1024]{1,0:T(4,128)}, u32[]{:S(2)}) copy-start(f32[4,1024]{1,0:T(4,128)} %param.13) | copy-start | bytes 49156

commit v3 on v2

--- a/solution.py
+++ b/solution.py
@@ -22,9 +22,8 @@
     padded,
     context,
     target,
-    weight,
+    small,
     stale,
-    trigger,
     summed_out,
     stale_out,
     norms_out,
@@ -61,6 +60,8 @@
     gz_r,
     gb_s,
     gb_r,
+    ge_s,
+    ge_r,
     ga_s,
     ga_r,
     gd_s,
@@ -114,6 +115,14 @@
             src_ref=src, dst_ref=dst, send_sem=s, recv_sem=r, device_id=to, device_id_type=MESH
         )
 
+    barrier = pltpu.get_barrier_semaphore()
+    greeted = [partner]
+    greeted += [x_peer(k) for k in range(1, NX)]
+    greeted += [y_peer(k) for k in range(1, NY)]
+    greeted += [z_peer(k) for k in range(1, NZ)]
+    for to in greeted:
+        pl.semaphore_signal(barrier, inc=1, device_id=to, device_id_type=MESH)
+
     context_in = pltpu.make_async_copy(context, cbuf.at[pl.ds(0, rows)], cin_sem)
     context_in.start()
     target_in = []
@@ -127,32 +136,7 @@
         target_in[j].start()
         stale_in[j].start()
 
-    barrier = pltpu.get_barrier_semaphore()
-    greeted = [partner]
-    greeted += [x_peer(k) for k in range(1, NX)]
-    greeted += [y_peer(k) for k in range(1, NY)]
-    greeted += [z_peer(k) for k in range(1, NZ)]
-    for to in greeted:
-        pl.semaphore_signal(barrier, inc=1, device_id=to, device_id_type=MESH)
-
-    group = 2 * NY * NZ * PIECE
-    place = lax.broadcasted_iota(jnp.int32, (group, group), 0)
-    natural = lax.broadcasted_iota(jnp.int32, (group, group), 1)
-
-    def natural_of(i):
-        ic, iy, iz, ir = i // 128, (i // 32) % 4, (i // 4) % 8, i % 4
-        return (iz % 4) * 64 + ic * 32 + (iz // 4) * 16 + iy * 4 + ir
-
-    perm[...] = jnp.where(natural == natural_of(place), 1.0, 0.0).astype(BF16)
-    perm_t[...] = jnp.where(place == natural_of(natural), 1.0, 0.0).astype(BF16)
-    own_low[...] = weight[...].astype(BF16)
-    tail = padded - rows
-    cbuf[pl.ds(rows, tail)] = jnp.zeros((tail, width), BF16)
-    ebuf[...] = jnp.zeros((padded, cols), BF16)
-    for j in range(CHUNKS):
-        tbuf[j, pl.ds(rows, tail)] = jnp.zeros((tail, cols), BF16)
-    sqacc[...] = jnp.zeros(sqacc.shape, F32)
-
+    own_low[...] = small[:PIECE].astype(BF16)
     pl.semaphore_wait(barrier, len(greeted))
 
     gz = []
@@ -160,6 +144,24 @@
         gz.append(remote(own_low, wz.at[z], gz_s.at[k - 1], gz_r.at[k - 1], z_peer(k)))
         gz[-1].start()
     wz[z] = own_low[...]
+
+    group = 2 * NY * NZ * PIECE
+    place = lax.broadcasted_iota(jnp.int32, (group, group), 0)
+    natural = lax.broadcasted_iota(jnp.int32, (group, group), 1)
+
+    def natural_of(i):
+        ic, iy, iz, ir = i // 128, (i // 32) % 4, (i // 4) % 8, i % 4
+        return (iz % 4) * 64 + ic * 32 + (iz // 4) * 16 + iy * 4 + ir
+
+    perm[...] = jnp.where(natural == natural_of(place), 1.0, 0.0).astype(BF16)
+    perm_t[...] = jnp.where(place == natural_of(natural), 1.0, 0.0).astype(BF16)
+    tail = padded - rows
+    cbuf[pl.ds(rows, tail)] = jnp.zeros((tail, width), BF16)
+    ebuf[...] = jnp.zeros((padded, cols), BF16)
+    for j in range(CHUNKS):
+        tbuf[j, pl.ds(rows, tail)] = jnp.zeros((tail, cols), BF16)
+    sqacc[...] = jnp.zeros(sqacc.shape, F32)
+
     context_in.wait()
 
     def turn(m, carry):
@@ -179,22 +181,34 @@
     own = wz32[...].astype(BF16)
     gb = []
     for j in range(CHUNKS):
-        wbuf[j, c, am, bm] = own[:, j * cols : (j + 1) * cols]
+        wbuf[j, c, am, 0] = own[:, j * cols : (j + 1) * cols]
     for j in range(CHUNKS):
         row = []
         for k in range(1, 4):
-            at = wbuf.at[j, c, am, bm]
             i = j * 3 + k - 1
-            row.append(remote(at, at, gb_s.at[i], gb_r.at[i], b_peer(lax.rem(bm + k, 4))))
+            row.append(
+                remote(
+                    wbuf.at[j, c, am, 0],
+                    wbuf.at[j, c, am, 4 - k],
+                    gb_s.at[i],
+                    gb_r.at[i],
+                    b_peer(lax.rem(bm + k, 4)),
+                )
+            )
             row[-1].start()
         gb.append(row)
+    ge = []
+    for k in range(1, 4):
+        at = wbuf.at[:, c, am, 0]
+        ge.append(remote(at, at, ge_s.at[k - 1], ge_r.at[k - 1], a_peer(lax.rem(am + k, 4))))
+        ge[-1].start()
     ga = []
     for j in range(CHUNKS):
         for copy in gb[j]:
             copy.wait_recv()
         row = []
         for k in range(1, 4):
-            at = wbuf.at[j, c, am]
+            at = wbuf.at[j, c, am, pl.ds(1, 3)]
             i = j * 3 + k - 1
             row.append(remote(at, at, ga_s.at[i], ga_r.at[i], a_peer(lax.rem(am + k, 4))))
             row[-1].start()
@@ -205,10 +219,15 @@
             at = pl.ds(g * group, group)
             sbuf[j, at] = jnp.dot(perm[...], sbuf[j, at], preferred_element_type=F32).astype(BF16)
     low = lax.broadcasted_iota(jnp.int32, (16, cols), 0) // PIECE
+    marks = small[PIECE : PIECE + 1, :128]
+    mark_at = lax.broadcasted_iota(jnp.int32, (1, 128), 1)
     for g in range(NX):
         flag = jnp.zeros((16, cols), F32)
         for i in range(4):
-            flag = jnp.where(low == i, trigger[0, g * 4 + i].astype(F32), flag)
+            one = jnp.sum(
+                jnp.where(mark_at == g * 4 + i, marks, 0.0), axis=1, keepdims=True
+            )
+            flag = jnp.where(low == i, one, flag)
         flags[g] = flag
 
     gd = []
@@ -226,15 +245,16 @@
     def forward(j):
         parts = []
         for g in range(NX):
-            parts += [wbuf[j, 0, g, b] for b in range(4)] + [wbuf[j, 1, b, g] for b in range(4)]
+            parts += [wbuf[j, 0, g, lax.rem(b - y + 4, 4)] for b in range(4)]
+            parts += [wbuf[j, 1, b, lax.rem(g - x + 4, 4)] for b in range(4)]
         low_part = jnp.concatenate(parts, axis=0)
         for m in range(4):
             at = pl.ds(m * tile, tile)
             out = jnp.dot(cbuf[at, :], low_part, preferred_element_type=F32)
             ebuf[at, :] = (out - tbuf[j, at].astype(F32)).astype(BF16)
 
-    def backward(j):
-        for g in range(NX):
+    def backward(j, first, last):
+        for g in range(first, last):
             at = pl.ds(g * group, group)
             grad = jnp.dot(ct[at, :], ebuf[...], preferred_element_type=F32) * scale
             mine = grad.reshape(16, 16, cols)
@@ -248,7 +268,7 @@
             fbuf[j, at] = fresh.reshape(group, cols).astype(BF16)
             for b in range(4):
                 half[j, 0, g, b] = chosen[b * 32 : (b + 1) * 32]
-                half[j, 1, b, g] = chosen[128 + b * 32 : 128 + (b + 1) * 32]
+                half[j, 1, g, b] = chosen[128 + b * 32 : 128 + (b + 1) * 32]
 
     def finish(j):
         for g in range(NX):
@@ -259,13 +279,25 @@
 
     rd, ra, rb, rz = [], [], [], []
 
-    def send_d(j):
-        rd.append(remote(half.at[j, 1 - c], drecv.at[j], rd_s.at[j], rd_r.at[j], partner))
-        rd[-1].start()
+    def send_d(j, first, last):
+        for g in range(first, last):
+            rd.append(
+                remote(
+                    half.at[j, 1 - c, g],
+                    drecv.at[j, g],
+                    rd_s.at[j * NX + g],
+                    rd_r.at[j * NX + g],
+                    partner,
+                )
+            )
+            rd[-1].start()
 
     def send_a(j):
-        rd[j].wait_recv()
-        asend[j] = (half[j, c].astype(F32) + drecv[j].astype(F32)).astype(BF16)
+        for g in range(NX):
+            rd[j * NX + g].wait_recv()
+            for b in range(4):
+                both = half[j, c, g, b].astype(F32) + drecv[j, g, b].astype(F32)
+                asend[j, g * (1 - c) + b * c, b * (1 - c) + g * c] = both.astype(BF16)
         row = []
         for k in range(1, 4):
             a = lax.rem(am + k, 4)
@@ -316,6 +348,8 @@
             row[-1].start()
         rz.append(row)
 
+    for copy in ge:
+        copy.wait_recv()
     to_partner(0)
     for j in range(CHUNKS):
         gd[j].wait_recv()
@@ -327,8 +361,14 @@
             send_a(j - 1)
         if j >= 3:
             send_b(j - 3)
-        backward(j)
-        send_d(j)
+        if j < CHUNKS - 1:
+            backward(j, 0, NX)
+            send_d(j, 0, NX)
+        else:
+            backward(j, 0, 2)
+            send_d(j, 0, 2)
+            backward(j, 2, NX)
+            send_d(j, 2, NX)
 
     def spread(src, bufs, at, peers, first):
         out = []
@@ -346,17 +386,17 @@
         preferred_element_type=F32,
     )
     sent = spread(nrm.at[0], nrm, 1, [partner], 0)
-    send_b(1)
-    send_z(0)
     send_a(3)
     sent[0].wait_recv()
     nx_buf[x] = nrm[0] + nrm[1]
     sent_x = spread(nx_buf.at[x], nx_buf, x, [x_peer(k) for k in range(1, NX)], 1)
-    send_z(1)
+    send_b(1)
+    send_z(0)
     finish(0)
     finish(1)
     send_b(2)
     finish(2)
+    send_z(1)
     finish(3)
     send_b(3)
     for copy in sent_x:
@@ -387,7 +427,7 @@
     lane = lax.broadcasted_iota(jnp.int32, (16, 128), 1)
     norms_out[...] = jnp.sum(jnp.where(row == lane, sums, 0.0), axis=0, keepdims=True)
 
-    for copy in gz + gd + rd + sent + sent_x + sent_y + sent_z:
+    for copy in gz + ge + gd + rd + sent + sent_x + sent_y + sent_z:
         copy.wait_send()
     for rows_of in (gb, ga, ra, rb, rz):
         for row in rows_of:
@@ -395,7 +435,7 @@
                 copy.wait_send()
 
 
-def step(context, target, weight, stale, trigger):
+def step(context, target, small, stale):
     rows, width = context.shape
     cols = width // CHUNKS
     padded = -(-rows // 128) * 128
@@ -409,7 +449,7 @@
             jax.ShapeDtypeStruct((1, width, width), BF16),
             jax.ShapeDtypeStruct((1, 128), F32),
         ),
-        in_specs=[hbm, hbm, vmem, hbm, pl.BlockSpec(memory_space=pltpu.SMEM)],
+        in_specs=[hbm, hbm, vmem, hbm],
         out_specs=(vmem, vmem, vmem),
         scratch_shapes=[
             pltpu.VMEM((padded, width), BF16),
@@ -445,12 +485,14 @@
             dma((NZ - 1,)),
             dma((CHUNKS * 3,)),
             dma((CHUNKS * 3,)),
+            dma((3,)),
+            dma((3,)),
             dma((CHUNKS * 3,)),
             dma((CHUNKS * 3,)),
             dma((CHUNKS,)),
             dma((CHUNKS,)),
-            dma((CHUNKS,)),
-            dma((CHUNKS,)),
+            dma((CHUNKS * NX,)),
+            dma((CHUNKS * NX,)),
             dma((CHUNKS * 3,)),
             dma((CHUNKS * 3,)),
             dma((CHUNKS * 3,)),
@@ -464,16 +506,76 @@
             collective_id=0, has_side_effects=True, vmem_limit_bytes=50 * 1024 * 1024
         ),
         name="step",
-    )(context, target, weight, stale, trigger)
+    )(context, target, small, stale)
+
+
+def update_kernel(
+    summed,
+    fresh,
+    sums,
+    weight,
+    aggregate,
+    moment,
+    second,
+    aggregate_out,
+    weight_out,
+    moment_out,
+    second_out,
+    stale_out,
+    norms_out,
+    rows_buf,
+    norms_buf,
+    sem,
+):
+    copies = [pltpu.make_async_copy(fresh, stale_out, sem.at[0])]
+    copies[0].start()
+    total = aggregate[...] + summed[...]
+    first = 0.9 * moment[...] + 0.1 * total
+    scaled = 0.999 * second[...] + 0.001 * total * total
+    old = weight[...]
+    rows_buf[0] = total
+    rows_buf[1] = old - 0.001 * (first / (jnp.sqrt(scaled) + 1e-08) + 0.05 * old)
+    rows_buf[2] = first
+    rows_buf[3] = scaled
+    for i in range(16):
+        norms_buf[i] = sums[0, i]
+    for i, out in enumerate((aggregate_out, weight_out, moment_out, second_out)):
+        copies.append(pltpu.make_async_copy(rows_buf.at[i], out, sem.at[1 + i]))
+    copies.append(pltpu.make_async_copy(norms_buf, norms_out, sem.at[5]))
+    for copy in copies[1:]:
+        copy.start()
+    for copy in copies:
+        copy.wait()
+
+
+def update(summed, fresh, sums, weight, aggregate, moment, second):
+    vmem = pl.BlockSpec(memory_space=pltpu.VMEM)
+    hbm = pl.BlockSpec(memory_space=pltpu.HBM)
+    smem = pl.BlockSpec(memory_space=pltpu.SMEM)
+    rows = jax.ShapeDtypeStruct(summed.shape, F32)
+    return pl.pallas_call(
+        update_kernel,
+        out_shape=(rows,) * 4
+        + (jax.ShapeDtypeStruct(fresh.shape, BF16), jax.ShapeDtypeStruct((16,), F32)),
+        in_specs=[vmem, vmem, smem] + [vmem] * 4,
+        out_specs=(hbm,) * 6,
+        scratch_shapes=[
+            pltpu.VMEM((4, *summed.shape), F32),
+            pltpu.SMEM((16,), F32),
+            pltpu.SemaphoreType.DMA((6,)),
+        ],
+        compiler_params=pltpu.CompilerParams(vmem_limit_bytes=16 * 1024 * 1024),
+        name="update",
+    )(summed, fresh, sums, weight, aggregate, moment, second)
 
 
 def body(context, target, weight, stale, trigger, aggregate, moment, second):
-    summed, stale_new, norms = step(context, target, weight, stale, trigger)
-    aggregate_new = aggregate + summed
-    moment_new = 0.9 * moment + 0.1 * aggregate_new
-    second_new = 0.999 * second + 0.001 * aggregate_new * aggregate_new
-    weight_new = weight - 0.001 * (moment_new / (jnp.sqrt(second_new) + 1e-08) + 0.05 * weight)
-    return (aggregate_new, weight_new, moment_new, second_new, stale_new, norms[0, :16])
+    above, width = weight.shape
+    marks = jnp.pad(trigger, ((above, 0), (0, width - trigger.shape[1]))).astype(F32)
+    at = lax.broadcasted_iota(jnp.int32, marks.shape, 0)
+    small = jnp.where(at < above, jnp.pad(weight, ((0, 1), (0, 0))), marks)
+    summed, fresh, sums = step(context, target, small, stale)
+    return update(summed, fresh, sums, weight, aggregate, moment, second)
 
 
 def solution(mesh):

time: 58.1 us -> 54.9 us (0.945)
  local copies, waits for them, and re-layouts: 3.21 us -> 0.02 us
    unnamed x11 -> x8, local copies, waits for them, and re-layouts: 2.69 us -> 0.02 us
    pallas_call x1, Pallas kernels: 53.3 us -> 50.9 us  [step(): pl.pallas_call(functools.partial(step_kernel, rows, padded), out_shape=(j...]
    pallas_call x0 -> x1, Pallas kernels: none -> 1.93 us  [update(): pl.pallas_call(update_kernel, out_shape=(rows,) * 4 + (jax.ShapeDtypeStru...]
    select_n x0 -> x1, other arithmetic: none -> 0.81 us  [body(): small = jnp.where(at < above, jnp.pad(weight, ((0, 1), (0, 0))), marks)]
    sub x1 -> x0, other arithmetic: 0.65 us -> none  [body(): weight - 0.001 * (moment_new / (jnp.sqrt(second_new) + 1e-08) + 0.05 * we...]
where the time goes in v3:
time: 54.9 us; the launch traced here: 54.3 us
  Pallas kernels  52.8 us (96%)
  other arithmetic  0.82 us (1%)
  between operations  0.69 us (1%)
    pallas_call x1, Pallas kernels, step(): pl.pallas_call(functools.partial(step_kernel, rows, padded), out_shape=(j...  50.9 us
    pallas_call x1, Pallas kernels, update(): pl.pallas_call(update_kernel, out_shape=(rows,) * 4 + (jax.ShapeDtypeStru...  1.93 us

profile of v3, /device:TPU:8, one launch (start us, length us, event | category | flops | bytes accessed | tf_op | source)
XLA Modules:
  0.0 54.3 jit_solution(13811987099504801902)
XLA Ops:
  0.6 0.8 %convert_select_fusion.small = f32[5,1024]{1,0:T(8,128)S(1)} fusion(s32[1,16]{1,0:T(1,128)} %param.12, f32[4,1024]{1,0:T(4,128)} %weight.1, pred[5]{0:T(512)(128)(4,1)S(1)} %iota_compare_fusion), kind=kLoop, calls=%fused_computation | loop fusion | flops 10240 | bytes 36933 | tf_op jit(solution)/shard_map/jit(_where)/select_n | solution.py:576
  1.5 0.0 copy-start
  1.5 0.0 copy-start.1
  1.5 0.0 copy-start.2
  1.5 0.0 copy-start.3
  1.5 50.9 %step.1 = (f32[4,1024]{1,0:T(4,128)S(1)}, bf16[1,1024,1024]{2,1,0:T(8,128)(2,1)S(1)}, f32[1,128]{1,0:T(1,128)S(1)}) custom-call(bf16[1576,1024]{1,0:T(8,128)(2,1)} %context.1, bf16[1576,1024]{1,0:T(8,128)(2,1)} %target.1, f32[5,1024]{1,0:T(8,128)S(1)} %convert_select_fusion.small, bf16[1,1024,1024]{2,1,0:T(8,128)(2,1)} %stale.1), custom_call_target="tpu_custom_call" | custom-call | tf_op jit(solution)/shard_map/step/pallas_call | solution.py:445
  52.4 0.0 copy-done
  52.4 0.0 copy-done.1
  52.4 0.0 copy-done.2
  52.4 0.0 copy-done.3
  52.4 1.9 %update.1 = (f32[4,1024]{1,0:T(4,128)}, f32[4,1024]{1,0:T(4,128)}, f32[4,1024]{1,0:T(4,128)}, f32[4,1024]{1,0:T(4,128)}, bf16[1,1024,1024]{2,1,0:T(8,128)(2,1)}, /*index=5*/f32[16]{0:T(128)}) custom-call(f32[4,1024]{1,0:T(4,128)S(1)} %get-tuple-element.9.summed, bf16[1,1024,1024]{2,1,0:T(8,128)(2,1)S(1)} %get-tuple-element.10.fresh, ...), custom_call_target="tpu_custom_call" | custom-call | tf_op jit(solution)/shard_map/update/pallas_call | solution.py:556
  (1 shorter events, 0.0 us)
Async XLA Ops:
  1.5 50.9 %copy-start = (f32[4,1024]{1,0:T(4,128)S(1)}, f32[4,1024]{1,0:T(4,128)}, u32[]{:S(2)}) copy-start(f32[4,1024]{1,0:T(4,128)} %weight.1) | copy-start | bytes 49156
  1.5 50.9 %copy-start.1 = (f32[4,1024]{1,0:T(4,128)S(1)}, f32[4,1024]{1,0:T(4,128)}, u32[]{:S(2)}) copy-start(f32[4,1024]{1,0:T(4,128)} %aggregate.1) | copy-start | bytes 49156
  1.5 50.9 %copy-start.2 = (f32[4,1024]{1,0:T(4,128)S(1)}, f32[4,1024]{1,0:T(4,128)}, u32[]{:S(2)}) copy-start(f32[4,1024]{1,0:T(4,128)} %moment.1) | copy-start | bytes 49156
  1.5 50.9 %copy-start.3 = (f32[4,1024]{1,0:T(4,128)S(1)}, f32[4,1024]{1,0:T(4,128)}, u32[]{:S(2)}) copy-start(f32[4,1024]{1,0:T(4,128)} %second.1) | copy-start | bytes 49156

commit v4 on v3

--- a/solution.py
+++ b/solution.py
@@ -14,6 +14,8 @@
 NX = 4
 NY = 4
 NZ = 8
+FAR4 = (2, 1, 3)
+FAR8 = (4, 3, 5, 2, 6, 1, 7)
 PIECE = 4
 
 
@@ -116,10 +118,10 @@
         )
 
     barrier = pltpu.get_barrier_semaphore()
-    greeted = [partner]
-    greeted += [x_peer(k) for k in range(1, NX)]
-    greeted += [y_peer(k) for k in range(1, NY)]
-    greeted += [z_peer(k) for k in range(1, NZ)]
+    greeted = [z_peer(k) for k in FAR8]
+    greeted += [x_peer(k) for k in FAR4]
+    greeted += [y_peer(k) for k in FAR4]
+    greeted += [partner]
     for to in greeted:
         pl.semaphore_signal(barrier, inc=1, device_id=to, device_id_type=MESH)
 
@@ -140,9 +142,14 @@
     pl.semaphore_wait(barrier, len(greeted))
 
     gz = []
-    for k in range(1, NZ):
-        gz.append(remote(own_low, wz.at[z], gz_s.at[k - 1], gz_r.at[k - 1], z_peer(k)))
-        gz[-1].start()
+    for h in range(2):
+        at = pl.ds(h * (width // 2), width // 2)
+        for k in FAR8:
+            i = h * 7 + k - 1
+            gz.append(
+                remote(own_low.at[:, at], wz.at[z, :, at], gz_s.at[i], gz_r.at[i], z_peer(k))
+            )
+            gz[-1].start()
     wz[z] = own_low[...]
 
     group = 2 * NY * NZ * PIECE
@@ -174,31 +181,32 @@
         return carry
 
     lax.fori_loop(0, padded // 128, turn, 0)
-    for copy in gz:
-        copy.wait_recv()
-    for i in range(NZ):
-        wz32[pl.ds(i * PIECE, PIECE), :] = wz[i].astype(F32)
-    own = wz32[...].astype(BF16)
     gb = []
-    for j in range(CHUNKS):
-        wbuf[j, c, am, 0] = own[:, j * cols : (j + 1) * cols]
-    for j in range(CHUNKS):
-        row = []
-        for k in range(1, 4):
-            i = j * 3 + k - 1
-            row.append(
-                remote(
-                    wbuf.at[j, c, am, 0],
-                    wbuf.at[j, c, am, 4 - k],
-                    gb_s.at[i],
-                    gb_r.at[i],
-                    b_peer(lax.rem(bm + k, 4)),
+    for h in range(2):
+        for copy in gz[h * 7 : (h + 1) * 7]:
+            copy.wait_recv()
+        at = pl.ds(h * (width // 2), width // 2)
+        for i in range(NZ):
+            wz32[pl.ds(i * PIECE, PIECE), at] = wz[i, :, at].astype(F32)
+        for j in range(h * 2, h * 2 + 2):
+            wbuf[j, c, am, 0] = wz32[:, j * cols : (j + 1) * cols].astype(BF16)
+        for j in range(h * 2, h * 2 + 2):
+            row = []
+            for k in FAR4:
+                i = j * 3 + k - 1
+                row.append(
+                    remote(
+                        wbuf.at[j, c, am, 0],
+                        wbuf.at[j, c, am, 4 - k],
+                        gb_s.at[i],
+                        gb_r.at[i],
+                        b_peer(lax.rem(bm + k, 4)),
+                    )
                 )
-            )
-            row[-1].start()
-        gb.append(row)
+                row[-1].start()
+            gb.append(row)
     ge = []
-    for k in range(1, 4):
+    for k in FAR4:
         at = wbuf.at[:, c, am, 0]
         ge.append(remote(at, at, ge_s.at[k - 1], ge_r.at[k - 1], a_peer(lax.rem(am + k, 4))))
         ge[-1].start()
@@ -240,7 +248,7 @@
         gd[-1].start()
 
     scale = 1.0 / rows
-    tile = padded // 4
+    tile = -(-rows // 48) * 16
 
     def forward(j):
         parts = []
@@ -248,7 +256,7 @@
             parts += [wbuf[j, 0, g, lax.rem(b - y + 4, 4)] for b in range(4)]
             parts += [wbuf[j, 1, b, lax.rem(g - x + 4, 4)] for b in range(4)]
         low_part = jnp.concatenate(parts, axis=0)
-        for m in range(4):
+        for m in range(3):
             at = pl.ds(m * tile, tile)
             out = jnp.dot(cbuf[at, :], low_part, preferred_element_type=F32)
             ebuf[at, :] = (out - tbuf[j, at].astype(F32)).astype(BF16)
@@ -299,7 +307,7 @@
                 both = half[j, c, g, b].astype(F32) + drecv[j, g, b].astype(F32)
                 asend[j, g * (1 - c) + b * c, b * (1 - c) + g * c] = both.astype(BF16)
         row = []
-        for k in range(1, 4):
+        for k in FAR4:
             a = lax.rem(am + k, 4)
             i = j * 3 + k - 1
             row.append(
@@ -316,7 +324,7 @@
             total = total + arecv[j, k].astype(F32)
         bsend[j] = total.astype(BF16)
         row = []
-        for k in range(1, 4):
+        for k in FAR4:
             b = lax.rem(bm + k, 4)
             i = j * 3 + k - 1
             row.append(
@@ -334,7 +342,7 @@
         for i in range(NZ):
             zsend[j, i] = total[i * PIECE : (i + 1) * PIECE].astype(BF16)
         row = []
-        for k in range(1, NZ):
+        for k in FAR8:
             i = j * 7 + k - 1
             row.append(
                 remote(
@@ -379,17 +387,21 @@
 
     pick = lax.broadcasted_iota(jnp.int32, (16, 64), 1) // PIECE
     pick = jnp.where(pick == lax.broadcasted_iota(jnp.int32, (16, 64), 0), 1.0, 0.0)
-    nrm[0] = jnp.dot(
+    block_sums = jnp.dot(
         pick.astype(F32),
         sqacc[...].reshape(64, 128),
         precision=lax.Precision.HIGHEST,
         preferred_element_type=F32,
     )
+    block_sums = jnp.broadcast_to(jnp.sum(block_sums, axis=1, keepdims=True), (16, 128))
+    row_at = lax.broadcasted_iota(jnp.int32, (16, 128), 0)
+    lane_at = lax.broadcasted_iota(jnp.int32, (16, 128), 1)
+    nrm[0] = jnp.sum(jnp.where(row_at == lane_at, block_sums, 0.0), axis=0, keepdims=True)
     sent = spread(nrm.at[0], nrm, 1, [partner], 0)
     send_a(3)
     sent[0].wait_recv()
     nx_buf[x] = nrm[0] + nrm[1]
-    sent_x = spread(nx_buf.at[x], nx_buf, x, [x_peer(k) for k in range(1, NX)], 1)
+    sent_x = spread(nx_buf.at[x], nx_buf, x, [x_peer(k) for k in FAR4], 1)
     send_b(1)
     send_z(0)
     finish(0)
@@ -402,13 +414,13 @@
     for copy in sent_x:
         copy.wait_recv()
     ny_buf[y] = (nx_buf[0] + nx_buf[1]) + (nx_buf[2] + nx_buf[3])
-    sent_y = spread(ny_buf.at[y], ny_buf, y, [y_peer(k) for k in range(1, NY)], 4)
+    sent_y = spread(ny_buf.at[y], ny_buf, y, [y_peer(k) for k in FAR4], 4)
     send_z(2)
     send_z(3)
     for copy in sent_y:
         copy.wait_recv()
     nz_buf[z] = (ny_buf[0] + ny_buf[1]) + (ny_buf[2] + ny_buf[3])
-    sent_z = spread(nz_buf.at[z], nz_buf, z, [z_peer(k) for k in range(1, NZ)], 7)
+    sent_z = spread(nz_buf.at[z], nz_buf, z, [z_peer(k) for k in FAR8], 7)
 
     for j in range(CHUNKS):
         for copy in rz[j]:
@@ -422,10 +434,7 @@
     every = nz_buf[0]
     for i in range(1, NZ):
         every = every + nz_buf[i]
-    sums = jnp.broadcast_to(jnp.sum(every, axis=1, keepdims=True), (16, 128))
-    row = lax.broadcasted_iota(jnp.int32, (16, 128), 0)
-    lane = lax.broadcasted_iota(jnp.int32, (16, 128), 1)
-    norms_out[...] = jnp.sum(jnp.where(row == lane, sums, 0.0), axis=0, keepdims=True)
+    norms_out[...] = every
 
     for copy in gz + ge + gd + rd + sent + sent_x + sent_y + sent_z:
         copy.wait_send()
@@ -474,15 +483,15 @@
             pltpu.VMEM((CHUNKS, NZ - 1, PIECE, cols), BF16),
             pltpu.VMEM((4, 16, 128), F32),
             pltpu.VMEM((4, 16, cols), F32),
-            pltpu.VMEM((2, 16, 128), F32),
-            pltpu.VMEM((NX, 16, 128), F32),
-            pltpu.VMEM((NY, 16, 128), F32),
-            pltpu.VMEM((NZ, 16, 128), F32),
+            pltpu.VMEM((2, 1, 128), F32),
+            pltpu.VMEM((NX, 1, 128), F32),
+            pltpu.VMEM((NY, 1, 128), F32),
+            pltpu.VMEM((NZ, 1, 128), F32),
             dma,
             dma((CHUNKS,)),
             dma((CHUNKS,)),
-            dma((NZ - 1,)),
-            dma((NZ - 1,)),
+            dma((2 * (NZ - 1),)),
+            dma((2 * (NZ - 1),)),
             dma((CHUNKS * 3,)),
             dma((CHUNKS * 3,)),
             dma((3,)),
@@ -524,11 +533,14 @@
     stale_out,
     norms_out,
     rows_buf,
+    sums_buf,
     norms_buf,
     sem,
 ):
     copies = [pltpu.make_async_copy(fresh, stale_out, sem.at[0])]
     copies[0].start()
+    sums_in = pltpu.make_async_copy(sums, sums_buf, sem.at[6])
+    sums_in.start()
     total = aggregate[...] + summed[...]
     first = 0.9 * moment[...] + 0.1 * total
     scaled = 0.999 * second[...] + 0.001 * total * total
@@ -537,13 +549,14 @@
     rows_buf[1] = old - 0.001 * (first / (jnp.sqrt(scaled) + 1e-08) + 0.05 * old)
     rows_buf[2] = first
     rows_buf[3] = scaled
-    for i in range(16):
-        norms_buf[i] = sums[0, i]
     for i, out in enumerate((aggregate_out, weight_out, moment_out, second_out)):
         copies.append(pltpu.make_async_copy(rows_buf.at[i], out, sem.at[1 + i]))
+        copies[-1].start()
+    sums_in.wait()
+    for i in range(16):
+        norms_buf[i] = sums_buf[0, i]
     copies.append(pltpu.make_async_copy(norms_buf, norms_out, sem.at[5]))
-    for copy in copies[1:]:
-        copy.start()
+    copies[-1].start()
     for copy in copies:
         copy.wait()
 
@@ -551,18 +564,18 @@
 def update(summed, fresh, sums, weight, aggregate, moment, second):
     vmem = pl.BlockSpec(memory_space=pltpu.VMEM)
     hbm = pl.BlockSpec(memory_space=pltpu.HBM)
-    smem = pl.BlockSpec(memory_space=pltpu.SMEM)
     rows = jax.ShapeDtypeStruct(summed.shape, F32)
     return pl.pallas_call(
         update_kernel,
         out_shape=(rows,) * 4
         + (jax.ShapeDtypeStruct(fresh.shape, BF16), jax.ShapeDtypeStruct((16,), F32)),
-        in_specs=[vmem, vmem, smem] + [vmem] * 4,
+        in_specs=[vmem] * 7,
         out_specs=(hbm,) * 6,
         scratch_shapes=[
             pltpu.VMEM((4, *summed.shape), F32),
+            pltpu.SMEM((1, 128), F32),
             pltpu.SMEM((16,), F32),
-            pltpu.SemaphoreType.DMA((6,)),
+            pltpu.SemaphoreType.DMA((7,)),
         ],
         compiler_params=pltpu.CompilerParams(vmem_limit_bytes=16 * 1024 * 1024),
         name="update",

time: 54.9 us -> 53.8 us (0.980)
  Pallas kernels: 52.8 us -> 51.9 us
where the time goes in v4:
time: 53.8 us; the launch traced here: 53.5 us
  Pallas kernels  51.9 us (96%)
  other arithmetic  0.82 us (2%)
  between operations  0.69 us (1%)
    pallas_call x1, Pallas kernels, step(): pl.pallas_call(functools.partial(step_kernel, rows, padded), out_shape=(j...  50.5 us
    pallas_call x1, Pallas kernels, update(): pl.pallas_call(update_kernel, out_shape=(rows,) * 4 + (jax.ShapeDtypeStru...  1.4 us

profile of v4, /device:TPU:8, one launch (start us, length us, event | category | flops | bytes accessed | tf_op | source)
XLA Modules:
  0.0 53.5 jit_solution(12722262258674690424)
XLA Ops:
  0.6 0.8 %convert_select_fusion.small = f32[5,1024]{1,0:T(8,128)S(1)} fusion(s32[1,16]{1,0:T(1,128)} %param.12, f32[4,1024]{1,0:T(4,128)} %weight.1, pred[5]{0:T(512)(128)(4,1)S(1)} %iota_compare_fusion), kind=kLoop, calls=%fused_computation | loop fusion | flops 10240 | bytes 36933 | tf_op jit(solution)/shard_map/jit(_where)/select_n | solution.py:589
  1.5 0.0 copy-start
  1.5 0.0 copy-start.1
  1.5 0.0 copy-start.2
  1.5 0.0 copy-start.3
  1.5 50.5 %step.1 = (f32[4,1024]{1,0:T(4,128)S(1)}, bf16[1,1024,1024]{2,1,0:T(8,128)(2,1)S(1)}, f32[1,128]{1,0:T(1,128)S(1)}) custom-call(bf16[1576,1024]{1,0:T(8,128)(2,1)} %context.1, bf16[1576,1024]{1,0:T(8,128)(2,1)} %target.1, f32[5,1024]{1,0:T(8,128)S(1)} %convert_select_fusion.small, bf16[1,1024,1024]{2,1,0:T(8,128)(2,1)} %stale.1), custom_call_target="tpu_custom_call" | custom-call | tf_op jit(solution)/shard_map/step/pallas_call | solution.py:454
  52.0 0.0 copy-done
  52.0 0.0 copy-done.1
  52.0 0.0 copy-done.2
  52.1 0.0 copy-done.3
  52.1 1.4 %update.1 = (f32[4,1024]{1,0:T(4,128)}, f32[4,1024]{1,0:T(4,128)}, f32[4,1024]{1,0:T(4,128)}, f32[4,1024]{1,0:T(4,128)}, bf16[1,1024,1024]{2,1,0:T(8,128)(2,1)}, /*index=5*/f32[16]{0:T(128)}) custom-call(f32[4,1024]{1,0:T(4,128)S(1)} %get-tuple-element.9.summed, bf16[1,1024,1024]{2,1,0:T(8,128)(2,1)S(1)} %get-tuple-element.10.fresh, ...), custom_call_target="tpu_custom_call" | custom-call | tf_op jit(solution)/shard_map/update/pallas_call | solution.py:568
  (1 shorter events, 0.0 us)
Async XLA Ops:
  1.5 50.6 %copy-start = (f32[4,1024]{1,0:T(4,128)S(1)}, f32[4,1024]{1,0:T(4,128)}, u32[]{:S(2)}) copy-start(f32[4,1024]{1,0:T(4,128)} %weight.1) | copy-start | bytes 49156
  1.5 50.6 %copy-start.1 = (f32[4,1024]{1,0:T(4,128)S(1)}, f32[4,1024]{1,0:T(4,128)}, u32[]{:S(2)}) copy-start(f32[4,1024]{1,0:T(4,128)} %aggregate.1) | copy-start | bytes 49156
  1.5 50.6 %copy-start.2 = (f32[4,1024]{1,0:T(4,128)S(1)}, f32[4,1024]{1,0:T(4,128)}, u32[]{:S(2)}) copy-start(f32[4,1024]{1,0:T(4,128)} %moment.1) | copy-start | bytes 49156
  1.5 50.6 %copy-start.3 = (f32[4,1024]{1,0:T(4,128)S(1)}, f32[4,1024]{1,0:T(4,128)}, u32[]{:S(2)}) copy-start(f32[4,1024]{1,0:T(4,128)} %second.1) | copy-start | bytes 49156
